TPU v7x, 32 devices: a whole 2x2x4 slice. The times are simulated.
32 devices in a mesh: gx: 2 (over x), gy: 4 (over y, core), gz: 4 (over z).
Axes of the slice: x: 2, y: 2, z: 4, core: 2. Of those that a mesh axis runs over, the one named last changes fastest.
Arguments:
- metric_pert: float32 [6, 32, 64, 512], P(None, 'gx', 'gy', 'gz'), may hold values from -1.8 to 1.8
- curvature: float32 [6, 32, 64, 512], P(None, 'gx', 'gy', 'gz'), may hold values from -6 to 6
- interp_weights: bfloat16 [2, 4, 32, 64, 4096], P('gx', 'gy', 'gz'), may hold values from -0.09375 to 0.09375
- point_ids: int32 [2, 4, 32, 64], P('gx', 'gy', 'gz'), may hold values from 0 to 6144, as said below
- theta: float32 [6144], replicated, may hold values from 0.05 to 3.09
- phi: float32 [6144], replicated, may hold values from -3.140625 to 3.140625
Outputs:
- psi4_field: bfloat16 [2, 32, 64, 512], P(None, 'gx', 'gy', 'gz')
- modes: float32 [3, 2, 77], replicated
Inputs may be any that keep to these rules, and one draw needn't show every extreme that they name: `point_ids`: the grid is a window of the extraction region that the spheres cross. A live entry names a sphere point; the value 6144 marks an empty slot, and each list holds its live entries first. The points of sphere s lie in the 9 consecutive block layers along the third dimension that begin at layer s * 10; each point belongs to one column (bx, by) and is listed in exactly two blocks of that column that are adjacent along the third dimension. Some block's list is full, every listing block holds at least 32 live entries, and blocks outside these layers list no point.
All inputs are finite; a program needn't handle non-finite values.
Results may differ from a plain program's by a relative error of at most 0.0032.
Values sent between devices are 32-bit elements; how exact they have to be, the bound alone decides.
No kernel may reach another device: no remote copies, remote signals or barrier semaphores. Data moves between devices by JAX's collectives and lax.ppermute only.
A program may use at most 64 MiB of HBM per device.

v0:
```python
import math
import jax
import jax.numpy as jnp
import numpy as np
from jax import lax
from jax.sharding import PartitionSpec as P

BLK = 16
PB = 64
PTS = 2048
SPHERES = 3
LMAX = 8
PAIRS = [[0, 1, 2], [1, 3, 4], [2, 4, 5]]


def padded_2(cells, sides, width):
    for axis, dim in sides:
        count = lax.axis_size(axis)
        ends = count - 1
        head = lax.slice_in_dim(cells, 0, width, axis=dim)
        tail = lax.slice_in_dim(cells, cells.shape[dim] - width, cells.shape[dim], axis=dim)
        cells = jnp.concatenate(
            [
                lax.ppermute(tail, axis, [(i, (i + 1) % count) for i in range(ends)]),
                cells,
                lax.ppermute(head, axis, [((i + 1) % count, i) for i in range(ends)]),
            ],
            axis=dim,
        )
    return cells


def build_table(degree_max):
    width = 2 * degree_max + 1
    columns = []
    orders = []
    for degree in range(2, degree_max + 1):
        for order in range(-degree, degree + 1):
            column = np.zeros(width * width)
            lead = (-1.0) ** order * math.sqrt(
                math.factorial(degree + order)
                * math.factorial(degree - order)
                * (2 * degree + 1)
                / (4.0 * math.pi * math.factorial(degree - 2) * math.factorial(degree + 2))
            )
            for step in range(0, degree + 3):
                lower = step - 2 - order
                if lower >= 0 and lower <= degree - 2:
                    value = (
                        lead
                        * math.comb(degree + 2, step)
                        * math.comb(degree - 2, lower)
                        * (-1.0) ** (degree - step + 2)
                    )
                    expo = 2 * step - 2 - order
                    column[expo * width + (2 * degree - expo)] += value
            columns.append(column)
            orders.append(order)
    return (np.stack(columns, 1), np.array(orders))


def project(sphere_vals, theta, phi, member):
    table, orders = build_table(LMAX)
    width = 2 * LMAX + 1
    cosine = jnp.cos(theta * 0.5)
    sine = jnp.sin(theta * 0.5)
    cos_pow = jnp.stack([cosine**power for power in range(width)], 1)
    sin_pow = jnp.stack([sine**power for power in range(width)], 1)
    grid_pow = (cos_pow[:, :, None] * sin_pow[:, None, :]).reshape(theta.shape[0], width * width)
    amplitude = jnp.dot(grid_pow, jnp.asarray(table, jnp.float32), precision=lax.Precision.HIGHEST)
    angle_m = phi[:, None] * jnp.asarray(orders, jnp.float32)[None, :]
    y_real = amplitude * jnp.cos(angle_m)
    y_imag = amplitude * jnp.sin(angle_m)
    left_re = member * sphere_vals[0][None, :]
    left_im = member * sphere_vals[1][None, :]
    highest = lax.Precision.HIGHEST
    real = jnp.dot(left_re, y_real, precision=highest) + jnp.dot(left_im, y_imag, precision=highest)
    imag = jnp.dot(left_im, y_real, precision=highest) - jnp.dot(left_re, y_imag, precision=highest)
    return jnp.stack([real, imag], 1) * (4.0 * math.pi / PTS)


def frame_terms(x_coord, y_coord, z_coord):
    x_full = x_coord[:, None, None]
    y_full = y_coord[None, :, None]
    z_full = z_coord[None, None, :]
    radial_xy = jnp.sqrt(x_full * x_full + y_full * y_full)
    radius = jnp.sqrt(radial_xy * radial_xy + z_full * z_full)
    cos_phi = x_full / radial_xy
    sin_phi = y_full / radial_xy
    cos_theta = z_full / radius
    sin_theta = radial_xy / radius
    e_theta = [cos_theta * cos_phi, cos_theta * sin_phi, -sin_theta]
    e_phi = [-sin_phi, cos_phi, 0.0 * cos_phi]
    return (e_theta, e_phi)


def weyl_scalar(padded, x_coord, y_coord, z_coord):
    extent = [x_coord.shape[0], y_coord.shape[0], z_coord.shape[0]]

    def moved(comp, axis, offset):
        index = [slice(2, 2 + count) for count in extent]
        index[axis] = slice(2 + offset, 2 + offset + extent[axis])
        return padded[comp][tuple(index)]

    def first(comp, axis):
        return (
            moved(comp, axis, -2)
            - 8.0 * moved(comp, axis, -1)
            + 8.0 * moved(comp, axis, 1)
            - moved(comp, axis, 2)
        ) / 12.0

    def second(comp, axis):
        return (
            -moved(comp, axis, -2)
            + 16.0 * moved(comp, axis, -1)
            - 30.0 * moved(comp, axis, 0)
            + 16.0 * moved(comp, axis, 1)
            - moved(comp, axis, 2)
        ) / 12.0

    kval = [moved(6 + comp, 0, 0) for comp in range(6)]
    trace = kval[0] + kval[3] + kval[5]
    electric = {}
    for row in range(3):
        for col in range(row, 3):
            comp = PAIRS[row][col]
            laplace = second(comp, 0) + second(comp, 1) + second(comp, 2)
            square = (
                kval[PAIRS[row][0]] * kval[PAIRS[0][col]]
                + kval[PAIRS[row][1]] * kval[PAIRS[1][col]]
                + kval[PAIRS[row][2]] * kval[PAIRS[2][col]]
            )
            value = -0.5 * laplace + trace * kval[comp] - square
            electric[row, col] = value
            electric[col, row] = value
    deriv = [[first(6 + comp, axis) for comp in range(6)] for axis in range(3)]
    curl = {}
    for row in range(3):
        one = (row + 1) % 3
        two = (row + 2) % 3
        for col in range(3):
            curl[row, col] = deriv[one][PAIRS[two][col]] - deriv[two][PAIRS[one][col]]
    e_theta, e_phi = frame_terms(x_coord, y_coord, z_coord)
    real = 0.0
    imag = 0.0
    for row in range(3):
        for col in range(3):
            magnetic = 0.5 * (curl[row, col] + curl[col, row])
            plus = 0.5 * (e_theta[row] * e_theta[col] - e_phi[row] * e_phi[col])
            cross = 0.5 * (e_theta[row] * e_phi[col] + e_phi[row] * e_theta[col])
            real = real + electric[row, col] * plus - magnetic * cross
            imag = imag - electric[row, col] * cross - magnetic * plus
    return jnp.stack([real, imag])


def shards(metric_pert, curvature, interp_weights, point_ids, theta, phi):
    fields = jnp.concatenate([metric_pert, curvature], 0)
    cells_x, cells_y, cells_z = (metric_pert.shape[1], metric_pert.shape[2], metric_pert.shape[3])
    whole_x = cells_x * lax.axis_size("gx")
    whole_y = cells_y * lax.axis_size("gy")
    whole_z = cells_z * lax.axis_size("gz")
    x_coord = (
        (lax.axis_index("gx") * cells_x + jnp.arange(cells_x)).astype(jnp.float32)
        + 0.5
        - whole_x / 2.0
    )
    y_coord = (
        (lax.axis_index("gy") * cells_y + jnp.arange(cells_y)).astype(jnp.float32)
        + 0.5
        - whole_y / 2.0
    )
    z_coord = (
        (lax.axis_index("gz") * cells_z + jnp.arange(cells_z)).astype(jnp.float32)
        + 0.5
        - whole_z / 2.0
    )
    padded = padded_2(fields, (("gx", 1), ("gy", 2), ("gz", 3)), 2)
    psi_local = weyl_scalar(padded, x_coord, y_coord, z_coord).astype(jnp.bfloat16)
    blocks_z = cells_z // BLK
    blocks = (
        psi_local.reshape(2, BLK, BLK, blocks_z, BLK)
        .transpose(3, 0, 1, 2, 4)
        .reshape(blocks_z, 2, BLK * BLK * BLK)
    )
    weights = interp_weights.reshape(blocks_z, PB, BLK * BLK * BLK)
    partial_value = jnp.einsum("bcn,bpn->bpc", blocks, weights, preferred_element_type=jnp.float32)
    slot_values = partial_value.reshape(-1, 2)
    point_list = point_ids.reshape(-1)
    total_points = SPHERES * PTS
    safe_list = jnp.minimum(point_list, total_points - 1)
    member = (point_list[None, :] // PTS == jnp.arange(SPHERES)[:, None]).astype(jnp.float32)
    local_modes = project(slot_values.T, theta[safe_list], phi[safe_list], member)
    modes = lax.psum(local_modes, ("gx", "gy", "gz"))
    return (psi_local, modes)


def solution(mesh):
    in_specs = (
        P(None, "gx", "gy", "gz"),
        P(None, "gx", "gy", "gz"),
        P("gx", "gy", "gz", None, None),
        P("gx", "gy", "gz", None),
        P(),
        P(),
    )
    out_specs = (P(None, "gx", "gy", "gz"), P())
    return jax.shard_map(shards, mesh=mesh, in_specs=in_specs, out_specs=out_specs, check_vma=False)
```

profile of v0, /device:TPU:0, one launch (start us, length us, event | category | flops | bytes accessed | tf_op | source)
XLA Modules:
  0.0 129.0 jit_solution(13485830494498539828)
XLA Ops:
  0.7 1.2 constant_dynamic-update-slice_fusion.1
  1.9 1.2 constant_dynamic-update-slice_fusion
  3.1 0.8 fusion.227
  3.9 4.9 %collective-permute-start = (f32[12,2,16,128]{3,2,1,0:T(8,128)}, f32[12,2,16,128]{3,2,1,0:T(8,128)S(1)}, u32[]{:S(2)}, u32[]{:S(2)}) collective-permute-start(f32[12,2,16,128]{3,2,1,0:T(8,128)} %get-tuple-element.43), channel_id=1, source_target_pairs={{0,16},{1,17},{2,18},{3,19},{4,20},{5,21},{6,22},{7,23},{8,24},{9,... | collective-permute-start | bytes 589832 | tf_op jit(solution)/shard_map/ppermute | solution.py:24
  8.8 1.3 %collective-permute-start.1 = (f32[12,2,16,128]{3,2,1,0:T(8,128)}, f32[12,2,16,128]{3,2,1,0:T(8,128)S(1)}, u32[]{:S(2)}, u32[]{:S(2)}) collective-permute-start(f32[12,2,16,128]{3,2,1,0:T(8,128)} %get-tuple-element.44), channel_id=1, source_target_pairs={{16,0},{17,1},{18,2},{19,3},{20,4},{21,5},{22,6},{23,7},{24,8},{25... | collective-permute-start | bytes 589832 | tf_op jit(solution)/shard_map/ppermute | solution.py:26
  10.1 0.1 broadcast_in_dim_reshape.3
  10.2 0.5 convert_add_fusion
  10.7 0.1 min.18
  10.8 3.1 %gather_fusion = f32[512]{0:T(512)S(1)} fusion(f32[6144]{0:T(1024)S(1)} %copy-done, s32[1024]{0:T(1024)S(1)} %pad_clamp_fusion), kind=kCustom, calls=%fused_computation | custom fusion | bytes 6144 | tf_op jit(solution)/shard_map/gather | solution.py:193
  14.1 0.1 stack.31
  14.1 0.1 stack.32
  14.2 0.1 broadcast_multiply_fusion
  14.3 0.1 mul.1636
  14.4 0.7 fusion.167
  15.2 2.0 %collective-permute-done.1 = f32[12,2,16,128]{3,2,1,0:T(8,128)S(1)} collective-permute-done((f32[12,2,16,128]{3,2,1,0:T(8,128)}, f32[12,2,16,128]{3,2,1,0:T(8,128)S(1)}, u32[]{:S(2)}, u32[]{:S(2)}) %collective-permute-start.1) | collective-permute-done | bytes 196640 | tf_op jit(solution)/shard_map/ppermute | solution.py:26
  17.2 0.2 pad_maximum_fusion.4
  17.4 1.3 %collective-permute-start.2 = (f32[12,20,2,128]{3,2,1,0:T(2,128)S(1)}, f32[12,20,2,128]{3,2,1,0:T(2,128)S(1)}, u32[]{:S(2)}, u32[]{:S(2)}) collective-permute-start(f32[12,20,2,128]{3,2,1,0:T(2,128)S(1)} %get-tuple-element.41), channel_id=1, source_target_pairs={{0,4},{4,8},{8,12},{1,5},{5,9},{9,13},{2,6},{6,10},{10,14},{3,7},{... | collective-permute-start | bytes 737288 | tf_op jit(solution)/shard_map/ppermute | solution.py:24
  18.7 1.3 %collective-permute-start.3 = (f32[12,20,2,128]{3,2,1,0:T(2,128)S(1)}, f32[12,20,2,128]{3,2,1,0:T(2,128)S(1)}, u32[]{:S(2)}, u32[]{:S(2)}) collective-permute-start(f32[12,20,2,128]{3,2,1,0:T(2,128)S(1)} %get-tuple-element.42), channel_id=1, source_target_pairs={{4,0},{8,4},{12,8},{5,1},{9,5},{13,9},{6,2},{10,6},{14,10},{7,3},{... | collective-permute-start | bytes 737288 | tf_op jit(solution)/shard_map/ppermute | solution.py:26
  20.0 1.6 %fusion.229 = f32[512,77]{0,1:T(8,128)S(1)} fusion(f32[512,289]{0,1:T(8,128)S(1)} %mul.1636, f32[289,77]{1,0:T(8,128)} %constant.111.clone), kind=kOutput, calls=%fused_computation.419 | convolution fusion | flops 136722432 | bytes 838580 | tf_op jit(solution)/shard_map/dot_general | solution.py:70
  21.6 2.3 %collective-permute-done.3 = f32[12,20,2,128]{3,2,1,0:T(2,128)S(1)} collective-permute-done((f32[12,20,2,128]{3,2,1,0:T(2,128)S(1)}, f32[12,20,2,128]{3,2,1,0:T(2,128)S(1)}, u32[]{:S(2)}, u32[]{:S(2)}) %collective-permute-start.3) | collective-permute-done | bytes 245792 | tf_op jit(solution)/shard_map/ppermute | solution.py:26
  23.9 1.4 %pad_maximum_fusion.1 = f32[12,20,20,128]{3,2,1,0:T(8,128)S(1)} fusion(f32[12,20,2,128]{3,2,1,0:T(2,128)S(1)} %collective-permute-done.3, f32[12,2,16,128]{3,2,1,0:T(8,128)} %copy-done.2, f32[12,16,16,128]{3,2,1,0:T(8,128)S(1)} %constant_dynamic-update-slice_fusion, f32[12,2,16,128]{3,2,1,0:T(8,128)S(1)} %collective-permute-done, ...), kind=kLoop, calls=%fused_computation.5 | loop fusion | flops 2457600 | bytes 4915200 | tf_op jit(solution)/shard_map/concatenate | solution.py:22
  25.3 3.5 %fusion.226 = (f32[12,20,20,2]{3,2,1,0:T(8,128)}, f32[12,20,20,2]{3,2,1,0:T(8,128)}) fusion(f32[12,20,20,128]{3,2,1,0:T(8,128)S(1)} %pad_maximum_fusion.1), kind=kLoop, calls=%fused_computation.416 | loop fusion | bytes 153600 | tf_op jit(solution)/shard_map/slice | solution.py:21
  28.8 3.0 %copy.32 = f32[12,20,20,2]{2,3,1,0:T(2,128)S(1)} copy(f32[12,20,20,2]{3,2,1,0:T(8,128)} %get-tuple-element.39) | data formatting | bytes 76800
  31.8 3.5 %collective-permute-start.4 = (f32[12,20,20,2]{2,3,1,0:T(2,128)S(1)}, f32[12,20,20,2]{2,3,1,0:T(2,128)S(1)}, u32[]{:S(2)}, u32[]{:S(2)}) collective-permute-start(f32[12,20,20,2]{2,3,1,0:T(2,128)S(1)} %copy.32), channel_id=1, source_target_pairs={{0,1},{1,2},{2,3},{4,5},{5,6},{6,7},{8,9},{9,10},{10,11},{12,13},{... | collective-permute-start | bytes 115208 | tf_op jit(solution)/shard_map/ppermute | solution.py:24
  35.3 3.0 %copy.33 = f32[12,20,20,2]{2,3,1,0:T(2,128)S(1)} copy(f32[12,20,20,2]{3,2,1,0:T(8,128)} %get-tuple-element.40) | data formatting | bytes 76800
  38.4 1.5 %collective-permute-start.5 = (f32[12,20,20,2]{2,3,1,0:T(2,128)S(1)}, f32[12,20,20,2]{2,3,1,0:T(2,128)}, u32[]{:S(2)}, u32[]{:S(2)}) collective-permute-start(f32[12,20,20,2]{2,3,1,0:T(2,128)S(1)} %copy.33), channel_id=1, source_target_pairs={{1,0},{2,1},{3,2},{5,4},{6,5},{7,6},{9,8},{10,9},{11,10},{13,12},{... | collective-permute-start | bytes 115208 | tf_op jit(solution)/shard_map/ppermute | solution.py:26
  39.9 3.1 %gather_fusion.1 = f32[512]{0:T(512)S(1)} fusion(f32[6144]{0:T(1024)S(1)} %copy-done.1, s32[1024]{0:T(1024)S(1)} %pad_clamp_fusion), kind=kCustom, calls=%fused_computation.1 | custom fusion | bytes 6144 | tf_op jit(solution)/shard_map/gather | solution.py:193
  43.0 2.8 %copy.26 = f32[12,20,20,2]{3,2,1,0:T(8,128)} copy(f32[12,20,20,2]{2,3,1,0:T(2,128)S(1)} %collective-permute-done.4) | data formatting | bytes 76800 | tf_op jit(solution)/shard_map/ppermute | solution.py:24
  45.9 0.7 collective-permute-done.5
  46.6 3.7 %copy.27 = f32[12,20,20,2]{3,2,1,0:T(8,128)} copy(f32[12,20,20,2]{2,3,1,0:T(2,128)} %collective-permute-done.5) | data formatting | bytes 76800 | tf_op jit(solution)/shard_map/ppermute | solution.py:26
  50.2 7.0 %pad_maximum_fusion = f32[12,20,20,132]{3,2,1,0:T(8,128)S(1)} fusion(f32[12,20,20,2]{3,2,1,0:T(8,128)} %copy.27, f32[12,20,2,128]{3,2,1,0:T(2,128)S(1)} %collective-permute-done.3, f32[12,2,16,128]{3,2,1,0:T(8,128)S(1)} %copy-done.3, f32[12,16,16,128]{3,2,1,0:T(8,128)S(1)} %constant_dynamic-update-slice_fusion, ...), kind=kLoop, calls=%fused_computation.2 | loop fusion | flops 3801600 | bytes 5068800 | tf_op jit(solution)/shard_map/concatenate | solution.py:22
  57.2 1.8 %slice_bitcast_fusion = (f32[20,20,132]{2,1,0:T(8,128)S(1)}, f32[20,20,132]{2,1,0:T(8,128)S(1)}, f32[20,20,132]{2,1,0:T(8,128)S(1)}, f32[20,20,132]{2,1,0:T(8,12...) fusion(f32[12,20,20,132]{3,2,1,0:T(8,128)S(1)} %pad_maximum_fusion), kind=kLoop, calls=%fused_computation.12 | loop fusion | bytes 5068800 | tf_op jit(solution)/shard_map/squeeze | solution.py:103
  59.0 14.9 %subtract_convert_fusion.1 = (bf16[16,16,128]{2,1,0:T(8,128)(2,1)S(1)}, f32[16,16,128]{2,1,0:T(8,128)S(1)}, f32[16,16,128]{2,1,0:T(8,128)}, f32[16,16,128]{2,1,0...) fusion(f32[16,16]{1,0:T(8,128)S(1)} %get-tuple-element.85, ...), kind=kLoop, calls=%fused_computation.304 | loop fusion | flops 12484608 | bytes 20526080 | tf_op jit(solution)/shard_map/convert.7
  74.0 1.9 %subtract_convert_fusion = bf16[16,16,128]{2,1,0:T(8,128)(2,1)S(1)} fusion(f32[16,16,128]{2,1,0:T(8,128)} %get-tuple-element.26, f32[16,16,128]{2,1,0:T(8,128)} %get-tuple-element.25, f32[16,16,128]{2,1,0:T(8,128)} %get-tuple-element.24, f32[16,16,128]{2,1,0:T(8,128)} %get-tuple-element.23, f32[16,16,128]{2,1,0:T(8,128)} %get-tuple-element.22, ...), kind=kLoop, calls=%fused_computation.303 | loop fusion | flops 2785280 | bytes 1651712 | tf_op jit(solution)/shard_map/convert.6
  75.9 0.4 stack.29
  76.3 0.1 copy.29
  76.4 0.4 stack.28
  76.8 0.2 maximum_bitcast_fusion
  77.1 1.1 reshape.879
  78.1 3.4 %fusion.2 = f32[8,64,2]{1,2,0:T(2,128)S(1)} fusion(bf16[8,2,4096]{2,1,0:T(2,128)(2,1)S(1)} %reshape.879, bf16[1,1,8,64,4096]{4,3,2,1,0:T(8,128)(2,1)} %param.10), kind=kOutput, calls=%fused_computation.6 | convolution fusion | flops 8388608 | bytes 4329472 | tf_op jit(solution)/shard_map/bcn,bpn->bpc/dot_general | solution.py:187
  81.5 0.1 reshape.881
  81.6 0.8 fusion.13
  82.4 0.8 fusion.11
  83.2 0.8 fusion.6
  84.1 0.8 fusion.5
  85.0 42.8 %psum.7 = f32[3,2,77]{2,0,1:T(4,128)S(1)} all-reduce(f32[3,2,77]{2,0,1:T(4,128)S(1)} %maximum_multiply_fusion), channel_id=1, replica_groups=mesh['gx'=2,'gy'=4,'gz'=4] {'gx','gy','gz'}, use_global_device_ids=true, to_apply=%region_0.1 | all-reduce | flops 462 | bytes 3696 | tf_op jit(solution)/shard_map/psum | solution.py:194
  127.8 0.6 copy.31
  128.4 0.7 pad_maximum_fusion.5
  (29 shorter events, 0.3 us)
Async XLA Ops:
  0.6 10.2 %copy-start = (f32[6144]{0:T(1024)S(1)}, f32[6144]{0:T(1024)}, u32[]{:S(2)}) copy-start(f32[6144]{0:T(1024)} %param.12) | copy-start | bytes 73732
  0.6 9.4 %copy-start.4 = (s32[1,1,8,64]{3,2,1,0:T(8,128)S(1)}, s32[1,1,8,64]{3,2,1,0:T(8,128)}, u32[]{:S(2)}) copy-start(s32[1,1,8,64]{3,2,1,0:T(8,128)} %param.11) | copy-start | bytes 6148
  3.9 11.3 %collective-permute-start = (f32[12,2,16,128]{3,2,1,0:T(8,128)}, f32[12,2,16,128]{3,2,1,0:T(8,128)S(1)}, u32[]{:S(2)}, u32[]{:S(2)}) collective-permute-start(f32[12,2,16,128]{3,2,1,0:T(8,128)} %get-tuple-element.43), channel_id=1, source_target_pairs={{0,16},{1,17},{2,18},{3,19},{4,20},{5,21},{6,22},{7,23},{8,24},{9,... | collective-permute-start | bytes 589832 | tf_op jit(solution)/shard_map/ppermute | solution.py:24
  8.8 8.5 %collective-permute-start.1 = (f32[12,2,16,128]{3,2,1,0:T(8,128)}, f32[12,2,16,128]{3,2,1,0:T(8,128)S(1)}, u32[]{:S(2)}, u32[]{:S(2)}) collective-permute-start(f32[12,2,16,128]{3,2,1,0:T(8,128)} %get-tuple-element.44), channel_id=1, source_target_pairs={{16,0},{17,1},{18,2},{19,3},{20,4},{21,5},{22,6},{23,7},{24,8},{25... | collective-permute-start | bytes 589832 | tf_op jit(solution)/shard_map/ppermute | solution.py:26
  17.2 1.5 %copy-start.2 = (f32[12,2,16,128]{3,2,1,0:T(8,128)}, f32[12,2,16,128]{3,2,1,0:T(8,128)S(1)}, u32[]{:S(2)}) copy-start(f32[12,2,16,128]{3,2,1,0:T(8,128)S(1)} %collective-permute-done.1) | copy-start | bytes 589828
  17.4 4.2 %collective-permute-start.2 = (f32[12,20,2,128]{3,2,1,0:T(2,128)S(1)}, f32[12,20,2,128]{3,2,1,0:T(2,128)S(1)}, u32[]{:S(2)}, u32[]{:S(2)}) collective-permute-start(f32[12,20,2,128]{3,2,1,0:T(2,128)S(1)} %get-tuple-element.41), channel_id=1, source_target_pairs={{0,4},{4,8},{8,12},{1,5},{5,9},{9,13},{2,6},{6,10},{10,14},{3,7},{... | collective-permute-start | bytes 737288 | tf_op jit(solution)/shard_map/ppermute | solution.py:24
  18.7 5.1 %collective-permute-start.3 = (f32[12,20,2,128]{3,2,1,0:T(2,128)S(1)}, f32[12,20,2,128]{3,2,1,0:T(2,128)S(1)}, u32[]{:S(2)}, u32[]{:S(2)}) collective-permute-start(f32[12,20,2,128]{3,2,1,0:T(2,128)S(1)} %get-tuple-element.42), channel_id=1, source_target_pairs={{4,0},{8,4},{12,8},{5,1},{9,5},{13,9},{6,2},{10,6},{14,10},{7,3},{... | collective-permute-start | bytes 737288 | tf_op jit(solution)/shard_map/ppermute | solution.py:26
  28.8 11.1 %copy-start.1 = (f32[6144]{0:T(1024)S(1)}, f32[6144]{0:T(1024)}, u32[]{:S(2)}) copy-start(f32[6144]{0:T(1024)} %param.13) | copy-start | bytes 73732
  31.8 11.2 %collective-permute-start.4 = (f32[12,20,20,2]{2,3,1,0:T(2,128)S(1)}, f32[12,20,20,2]{2,3,1,0:T(2,128)S(1)}, u32[]{:S(2)}, u32[]{:S(2)}) collective-permute-start(f32[12,20,20,2]{2,3,1,0:T(2,128)S(1)} %copy.32), channel_id=1, source_target_pairs={{0,1},{1,2},{2,3},{4,5},{5,6},{6,7},{8,9},{9,10},{10,11},{12,13},{... | collective-permute-start | bytes 115208 | tf_op jit(solution)/shard_map/ppermute | solution.py:24
  38.4 8.2 %collective-permute-start.5 = (f32[12,20,20,2]{2,3,1,0:T(2,128)S(1)}, f32[12,20,20,2]{2,3,1,0:T(2,128)}, u32[]{:S(2)}, u32[]{:S(2)}) collective-permute-start(f32[12,20,20,2]{2,3,1,0:T(2,128)S(1)} %copy.33), channel_id=1, source_target_pairs={{1,0},{2,1},{3,2},{5,4},{6,5},{7,6},{9,8},{10,9},{11,10},{13,12},{... | collective-permute-start | bytes 115208 | tf_op jit(solution)/shard_map/ppermute | solution.py:26
  43.0 7.2 %copy-start.3 = (f32[12,2,16,128]{3,2,1,0:T(8,128)S(1)}, f32[12,2,16,128]{3,2,1,0:T(8,128)}, u32[]{:S(2)}) copy-start(f32[12,2,16,128]{3,2,1,0:T(8,128)} %copy-done.2) | copy-start | bytes 589828
  77.0 4.6 %copy-start.5 = (f32[77]{0:T(128)S(1)}, f32[77]{0:T(128)}, u32[]{:S(2)}) copy-start(f32[77]{0:T(128)} %constant.112.clone) | copy-start | bytes 928
where the time goes:
time: 130 us; the launch traced here: 129 us
  blocking collectives  42.8 us (33%)
  local copies, waits for them, and re-layouts  30.5 us (23%)
  other arithmetic  27.8 us (21%)
  starting transfers between devices  13.7 us (11%)
  matrix products  8.25 us (6%)
  waiting for transfers between devices  4.98 us (4%)
    psum x1, blocking collectives, shards(): modes = lax.psum(local_modes, ('gx', 'gy', 'gz'))  42.8 us
    another operation x2, other arithmetic  16.9 us
    ppermute x3, starting transfers between devices, padded_2(): lax.ppermute(tail, axis, [(i, (i + 1) % count) for i in range(ends)])  9.67 us
    concatenate x2, other arithmetic, padded_2(): jnp.concatenate([lax.ppermute(tail, axis, [(i, (i + 1) % count) for i in...  8.35 us
    unnamed x16, local copies, waits for them, and re-layouts  7.91 us
    ppermute x3, waiting for transfers between devices, padded_2(): lax.ppermute(head, axis, [((i + 1) % count, i) for i in range(ends)])  4.97 us
    slice x2, local copies, waits for them, and re-layouts, padded_2(): lax.slice_in_dim(cells, cells.shape[dim] - width, cells.shape[dim], axis=...  4.32 us
    ppermute x3, starting transfers between devices, padded_2(): lax.ppermute(head, axis, [((i + 1) % count, i) for i in range(ends)])  4.06 us
  transfers between devices with their start and end apart: 6, of which 3 were waited for; matrix products, arithmetic and copies ran while one was open for 12% of the time, Pallas kernels for 0%

commit v1 on v0

--- a/solution.py
+++ b/solution.py
@@ -191,7 +191,7 @@
     safe_list = jnp.minimum(point_list, total_points - 1)
     member = (point_list[None, :] // PTS == jnp.arange(SPHERES)[:, None]).astype(jnp.float32)
     local_modes = project(slot_values.T, theta[safe_list], phi[safe_list], member)
-    modes = lax.psum(local_modes, ("gx", "gy", "gz"))
+    modes = jnp.sum(lax.all_gather(local_modes, ("gx", "gy", "gz")), axis=0)
     return (psi_local, modes)
 
 

time: 130 us -> 155 us (1.19)
  blocking collectives: 42.8 us -> 68.1 us
    all_gather x0 -> x1, blocking collectives: none -> 68.1 us  [shards(): modes = jnp.sum(lax.all_gather(local_modes, ('gx', 'gy', 'gz')), axis=0)]
    psum x1 -> x0, blocking collectives: 42.8 us -> none  [shards(): modes = lax.psum(local_modes, ('gx', 'gy', 'gz'))]
    unnamed x16 -> x15, local copies, waits for them, and re-layouts: 7.91 us -> 7.33 us
  transfers between devices with their start and end apart: 6 -> 6, of which waited for: 3 -> 3; matrix products, arithmetic and copies ran while one was open for 12% -> 10% of each run, Pallas kernels for 0% -> 0%
where the time goes in v1:
time: 155 us; the launch traced here: 154 us
  blocking collectives  68.1 us (44%)
  local copies, waits for them, and re-layouts  29.9 us (19%)
  other arithmetic  28.4 us (18%)
  starting transfers between devices  13.7 us (9%)
  matrix products  8.25 us (5%)
  waiting for transfers between devices  4.98 us (3%)
    all_gather x1, blocking collectives, shards(): modes = jnp.sum(lax.all_gather(local_modes, ('gx', 'gy', 'gz')), axis=0)  68.1 us
    another operation x2, other arithmetic  16.9 us
    ppermute x3, starting transfers between devices, padded_2(): lax.ppermute(tail, axis, [(i, (i + 1) % count) for i in range(ends)])  9.67 us
    concatenate x2, other arithmetic, padded_2(): jnp.concatenate([lax.ppermute(tail, axis, [(i, (i + 1) % count) for i in...  8.35 us
    unnamed x15, local copies, waits for them, and re-layouts  7.33 us
    ppermute x3, waiting for transfers between devices, padded_2(): lax.ppermute(head, axis, [((i + 1) % count, i) for i in range(ends)])  4.97 us
    slice x2, local copies, waits for them, and re-layouts, padded_2(): lax.slice_in_dim(cells, cells.shape[dim] - width, cells.shape[dim], axis=...  4.32 us
    ppermute x3, starting transfers between devices, padded_2(): lax.ppermute(head, axis, [((i + 1) % count, i) for i in range(ends)])  4.06 us
  transfers between devices with their start and end apart: 6, of which 3 were waited for; matrix products, arithmetic and copies ran while one was open for 10% of the time, Pallas kernels for 0%

profile of v1, /device:TPU:0, one launch (start us, length us, event | category | flops | bytes accessed | tf_op | source)
XLA Modules:
  0.0 154.4 jit_solution(15635720790880607436)
XLA Ops:
  0.7 1.2 constant_dynamic-update-slice_fusion.1
  1.9 1.2 constant_dynamic-update-slice_fusion
  3.1 0.8 fusion.227
  3.9 4.9 %collective-permute-start = (f32[12,2,16,128]{3,2,1,0:T(8,128)}, f32[12,2,16,128]{3,2,1,0:T(8,128)S(1)}, u32[]{:S(2)}, u32[]{:S(2)}) collective-permute-start(f32[12,2,16,128]{3,2,1,0:T(8,128)} %get-tuple-element.39), channel_id=1, source_target_pairs={{0,16},{1,17},{2,18},{3,19},{4,20},{5,21},{6,22},{7,23},{8,24},{9,... | collective-permute-start | bytes 589832 | tf_op jit(solution)/shard_map/ppermute | solution.py:24
  8.8 1.3 collective-permute-start.1
  10.1 0.1 broadcast_in_dim_reshape.3
  10.2 0.5 convert_add_fusion
  10.7 0.1 min.18
  10.8 3.1 %gather_fusion = f32[512]{0:T(512)S(1)} fusion(f32[6144]{0:T(1024)S(1)} %copy-done, s32[1024]{0:T(1024)S(1)} %pad_clamp_fusion), kind=kCustom, calls=%fused_computation | custom fusion | bytes 6144 | tf_op jit(solution)/shard_map/gather | solution.py:193
  14.1 0.1 stack.31
  14.1 0.1 stack.32
  14.2 0.1 broadcast_multiply_fusion
  14.3 0.1 mul.1643
  14.4 0.7 fusion.167
  15.2 2.0 %collective-permute-done.1 = f32[12,2,16,128]{3,2,1,0:T(8,128)S(1)} collective-permute-done((f32[12,2,16,128]{3,2,1,0:T(8,128)}, f32[12,2,16,128]{3,2,1,0:T(8,128)S(1)}, u32[]{:S(2)}, u32[]{:S(2)}) %collective-permute-start.1) | collective-permute-done | bytes 196640 | tf_op jit(solution)/shard_map/ppermute | solution.py:26
  17.2 0.2 pad_maximum_fusion.4
  17.4 1.3 collective-permute-start.2
  18.7 1.3 collective-permute-start.3
  20.0 1.6 %fusion.229 = f32[512,77]{0,1:T(8,128)S(1)} fusion(f32[512,289]{0,1:T(8,128)S(1)} %mul.1643, f32[289,77]{1,0:T(8,128)} %constant.112.clone), kind=kOutput, calls=%fused_computation.419 | convolution fusion | flops 136722432 | bytes 838580 | tf_op jit(solution)/shard_map/dot_general | solution.py:70
  21.6 2.3 %collective-permute-done.3 = f32[12,20,2,128]{3,2,1,0:T(2,128)S(1)} collective-permute-done((f32[12,20,2,128]{3,2,1,0:T(2,128)S(1)}, f32[12,20,2,128]{3,2,1,0:T(2,128)S(1)}, u32[]{:S(2)}, u32[]{:S(2)}) %collective-permute-start.3) | collective-permute-done | bytes 245792 | tf_op jit(solution)/shard_map/ppermute | solution.py:26
  23.9 1.4 pad_maximum_fusion.1
  25.3 3.5 %fusion.226 = (f32[12,20,20,2]{3,2,1,0:T(8,128)}, f32[12,20,20,2]{3,2,1,0:T(8,128)}) fusion(f32[12,20,20,128]{3,2,1,0:T(8,128)S(1)} %pad_maximum_fusion.1), kind=kLoop, calls=%fused_computation.416 | loop fusion | bytes 153600 | tf_op jit(solution)/shard_map/slice | solution.py:21
  28.8 3.0 %copy.35 = f32[12,20,20,2]{2,3,1,0:T(2,128)S(1)} copy(f32[12,20,20,2]{3,2,1,0:T(8,128)} %get-tuple-element.35) | data formatting | bytes 76800
  31.8 3.5 %collective-permute-start.4 = (f32[12,20,20,2]{2,3,1,0:T(2,128)S(1)}, f32[12,20,20,2]{2,3,1,0:T(2,128)S(1)}, u32[]{:S(2)}, u32[]{:S(2)}) collective-permute-start(f32[12,20,20,2]{2,3,1,0:T(2,128)S(1)} %copy.35), channel_id=1, source_target_pairs={{0,1},{1,2},{2,3},{4,5},{5,6},{6,7},{8,9},{9,10},{10,11},{12,13},{... | collective-permute-start | bytes 115208 | tf_op jit(solution)/shard_map/ppermute | solution.py:24
  35.3 3.0 %copy.36 = f32[12,20,20,2]{2,3,1,0:T(2,128)S(1)} copy(f32[12,20,20,2]{3,2,1,0:T(8,128)} %get-tuple-element.36) | data formatting | bytes 76800
  38.4 1.5 collective-permute-start.5
  39.9 3.1 %gather_fusion.1 = f32[512]{0:T(512)S(1)} fusion(f32[6144]{0:T(1024)S(1)} %copy-done.1, s32[1024]{0:T(1024)S(1)} %pad_clamp_fusion), kind=kCustom, calls=%fused_computation.1 | custom fusion | bytes 6144 | tf_op jit(solution)/shard_map/gather | solution.py:193
  43.0 2.8 %copy.26 = f32[12,20,20,2]{3,2,1,0:T(8,128)} copy(f32[12,20,20,2]{2,3,1,0:T(2,128)S(1)} %collective-permute-done.4) | data formatting | bytes 76800 | tf_op jit(solution)/shard_map/ppermute | solution.py:24
  45.9 0.7 collective-permute-done.5
  46.6 3.7 %copy.27 = f32[12,20,20,2]{3,2,1,0:T(8,128)} copy(f32[12,20,20,2]{2,3,1,0:T(2,128)} %collective-permute-done.5) | data formatting | bytes 76800 | tf_op jit(solution)/shard_map/ppermute | solution.py:26
  50.2 7.0 %pad_maximum_fusion = f32[12,20,20,132]{3,2,1,0:T(8,128)S(1)} fusion(f32[12,20,20,2]{3,2,1,0:T(8,128)} %copy.27, f32[12,20,2,128]{3,2,1,0:T(2,128)S(1)} %collective-permute-done.3, f32[12,2,16,128]{3,2,1,0:T(8,128)S(1)} %copy-done.3, f32[12,16,16,128]{3,2,1,0:T(8,128)S(1)} %constant_dynamic-update-slice_fusion, ...), kind=kLoop, calls=%fused_computation.2 | loop fusion | flops 3801600 | bytes 5068800 | tf_op jit(solution)/shard_map/concatenate | solution.py:22
  57.2 1.8 %slice_bitcast_fusion = (f32[20,20,132]{2,1,0:T(8,128)S(1)}, f32[20,20,132]{2,1,0:T(8,128)S(1)}, f32[20,20,132]{2,1,0:T(8,128)S(1)}, f32[20,20,132]{2,1,0:T(8,12...) fusion(f32[12,20,20,132]{3,2,1,0:T(8,128)S(1)} %pad_maximum_fusion), kind=kLoop, calls=%fused_computation.12 | loop fusion | bytes 5068800 | tf_op jit(solution)/shard_map/squeeze | solution.py:103
  59.0 14.9 %subtract_convert_fusion.1 = (bf16[16,16,128]{2,1,0:T(8,128)(2,1)S(1)}, f32[16,16,128]{2,1,0:T(8,128)S(1)}, f32[16,16,128]{2,1,0:T(8,128)}, f32[16,16,128]{2,1,0...) fusion(f32[16,16]{1,0:T(8,128)S(1)} %get-tuple-element.81, ...), kind=kLoop, calls=%fused_computation.304 | loop fusion | flops 12484608 | bytes 20526080 | tf_op jit(solution)/shard_map/convert.7
  74.0 1.9 %subtract_convert_fusion = bf16[16,16,128]{2,1,0:T(8,128)(2,1)S(1)} fusion(f32[16,16,128]{2,1,0:T(8,128)} %get-tuple-element.22, f32[16,16,128]{2,1,0:T(8,128)} %get-tuple-element.21, f32[16,16,128]{2,1,0:T(8,128)} %get-tuple-element.20, f32[16,16,128]{2,1,0:T(8,128)} %get-tuple-element.19, f32[16,16,128]{2,1,0:T(8,128)} %get-tuple-element.18, ...), kind=kLoop, calls=%fused_computation.303 | loop fusion | flops 2785280 | bytes 1651712 | tf_op jit(solution)/shard_map/convert.6
  75.9 0.4 stack.29
  76.3 0.1 copy.29
  76.4 0.4 stack.28
  76.8 0.2 maximum_bitcast_fusion
  77.1 1.1 reshape.910
  78.1 3.4 %fusion.2 = f32[8,64,2]{1,2,0:T(2,128)S(1)} fusion(bf16[8,2,4096]{2,1,0:T(2,128)(2,1)S(1)} %reshape.910, bf16[1,1,8,64,4096]{4,3,2,1,0:T(8,128)(2,1)} %param.10), kind=kOutput, calls=%fused_computation.6 | convolution fusion | flops 8388608 | bytes 4329472 | tf_op jit(solution)/shard_map/bcn,bpn->bpc/dot_general | solution.py:187
  81.5 0.1 reshape.912
  81.6 0.8 fusion.13
  82.4 0.8 fusion.11
  83.2 0.8 fusion.6
  84.1 0.8 fusion.5
  85.0 68.1 %all_gather.4 = f32[32,3,2,77]{3,2,1,0:T(2,128)S(1)} all-gather(f32[1,3,2,77]{3,2,1,0:T(2,128)S(1)} %copy.31), channel_id=1, replica_groups=mesh['gx'=2,'gy'=4,'gz'=4] {'gx','gy','gz'}, dimensions={0}, use_global_device_ids=true | all-gather | bytes 60984 | tf_op jit(solution)/shard_map/all_gather | solution.py:194
  153.1 0.6 reduce_sum.9
  153.8 0.7 pad_maximum_fusion.5
  (30 shorter events, 0.3 us)
Async XLA Ops:
  0.6 10.2 %copy-start = (f32[6144]{0:T(1024)S(1)}, f32[6144]{0:T(1024)}, u32[]{:S(2)}) copy-start(f32[6144]{0:T(1024)} %param.12) | copy-start | bytes 73732
  0.6 9.4 %copy-start.4 = (s32[1,1,8,64]{3,2,1,0:T(8,128)S(1)}, s32[1,1,8,64]{3,2,1,0:T(8,128)}, u32[]{:S(2)}) copy-start(s32[1,1,8,64]{3,2,1,0:T(8,128)} %param.11) | copy-start | bytes 6148
  3.9 11.3 %collective-permute-start = (f32[12,2,16,128]{3,2,1,0:T(8,128)}, f32[12,2,16,128]{3,2,1,0:T(8,128)S(1)}, u32[]{:S(2)}, u32[]{:S(2)}) collective-permute-start(f32[12,2,16,128]{3,2,1,0:T(8,128)} %get-tuple-element.39), channel_id=1, source_target_pairs={{0,16},{1,17},{2,18},{3,19},{4,20},{5,21},{6,22},{7,23},{8,24},{9,... | collective-permute-start | bytes 589832 | tf_op jit(solution)/shard_map/ppermute | solution.py:24
  8.8 8.5 %collective-permute-start.1 = (f32[12,2,16,128]{3,2,1,0:T(8,128)}, f32[12,2,16,128]{3,2,1,0:T(8,128)S(1)}, u32[]{:S(2)}, u32[]{:S(2)}) collective-permute-start(f32[12,2,16,128]{3,2,1,0:T(8,128)} %get-tuple-element.40), channel_id=1, source_target_pairs={{16,0},{17,1},{18,2},{19,3},{20,4},{21,5},{22,6},{23,7},{24,8},{25... | collective-permute-start | bytes 589832 | tf_op jit(solution)/shard_map/ppermute | solution.py:26
  17.2 1.5 copy-start.2
  17.4 4.2 %collective-permute-start.2 = (f32[12,20,2,128]{3,2,1,0:T(2,128)S(1)}, f32[12,20,2,128]{3,2,1,0:T(2,128)S(1)}, u32[]{:S(2)}, u32[]{:S(2)}) collective-permute-start(f32[12,20,2,128]{3,2,1,0:T(2,128)S(1)} %get-tuple-element.37), channel_id=1, source_target_pairs={{0,4},{4,8},{8,12},{1,5},{5,9},{9,13},{2,6},{6,10},{10,14},{3,7},{... | collective-permute-start | bytes 737288 | tf_op jit(solution)/shard_map/ppermute | solution.py:24
  18.7 5.1 %collective-permute-start.3 = (f32[12,20,2,128]{3,2,1,0:T(2,128)S(1)}, f32[12,20,2,128]{3,2,1,0:T(2,128)S(1)}, u32[]{:S(2)}, u32[]{:S(2)}) collective-permute-start(f32[12,20,2,128]{3,2,1,0:T(2,128)S(1)} %get-tuple-element.38), channel_id=1, source_target_pairs={{4,0},{8,4},{12,8},{5,1},{9,5},{13,9},{6,2},{10,6},{14,10},{7,3},{... | collective-permute-start | bytes 737288 | tf_op jit(solution)/shard_map/ppermute | solution.py:26
  28.8 11.1 %copy-start.1 = (f32[6144]{0:T(1024)S(1)}, f32[6144]{0:T(1024)}, u32[]{:S(2)}) copy-start(f32[6144]{0:T(1024)} %param.13) | copy-start | bytes 73732
  31.8 11.2 %collective-permute-start.4 = (f32[12,20,20,2]{2,3,1,0:T(2,128)S(1)}, f32[12,20,20,2]{2,3,1,0:T(2,128)S(1)}, u32[]{:S(2)}, u32[]{:S(2)}) collective-permute-start(f32[12,20,20,2]{2,3,1,0:T(2,128)S(1)} %copy.35), channel_id=1, source_target_pairs={{0,1},{1,2},{2,3},{4,5},{5,6},{6,7},{8,9},{9,10},{10,11},{12,13},{... | collective-permute-start | bytes 115208 | tf_op jit(solution)/shard_map/ppermute | solution.py:24
  38.4 8.2 %collective-permute-start.5 = (f32[12,20,20,2]{2,3,1,0:T(2,128)S(1)}, f32[12,20,20,2]{2,3,1,0:T(2,128)}, u32[]{:S(2)}, u32[]{:S(2)}) collective-permute-start(f32[12,20,20,2]{2,3,1,0:T(2,128)S(1)} %copy.36), channel_id=1, source_target_pairs={{1,0},{2,1},{3,2},{5,4},{6,5},{7,6},{9,8},{10,9},{11,10},{13,12},{... | collective-permute-start | bytes 115208 | tf_op jit(solution)/shard_map/ppermute | solution.py:26
  43.0 7.2 %copy-start.3 = (f32[12,2,16,128]{3,2,1,0:T(8,128)S(1)}, f32[12,2,16,128]{3,2,1,0:T(8,128)}, u32[]{:S(2)}) copy-start(f32[12,2,16,128]{3,2,1,0:T(8,128)} %copy-done.2) | copy-start | bytes 589828
  77.0 4.6 %copy-start.5 = (f32[77]{0:T(128)S(1)}, f32[77]{0:T(128)}, u32[]{:S(2)}) copy-start(f32[77]{0:T(128)} %constant.113.clone) | copy-start | bytes 928
